TPU v7x, 512 devices: a whole 4x8x8 slice. The times are simulated.
512 devices in a mesh: sp: 64 (over z, y_hi, core), dp: 8 (over y_lo, x).
Axes of the slice: x: 4, y: 8 (y_hi: 4, y_lo: 2; y = y_hi * 2 + y_lo), z: 8, core: 2. Of those that a mesh axis runs over, the one named last changes fastest.
Arguments:
- query_proj: bfloat16 [65536, 8192], P(('dp', 'sp')), parts along dimension 0, may hold values from -64 to 64
- key_projection: bfloat16 [65536, 1024], P(('dp', 'sp')), parts along dimension 0, may hold values from -64 to 64
- value_projection: bfloat16 [65536, 1024], P(('dp', 'sp')), parts along dimension 0, may hold values from -12 to 12
- query_gain: float32 [128], replicated, may hold values from 1 to 5
- key_norm_gain: float32 [128], replicated, may hold values from 1 to 5
- positions: int32 [65536], P(('dp', 'sp')), parts along dimension 0, may hold values from 0 to 5118, as said below
- doc_start: int32 [65536], P(('dp', 'sp')), parts along dimension 0, may hold values from 0 to 8191, as said below
Outputs:
- attention: bfloat16 [65536, 8192], P(('dp', 'sp')), parts along dimension 0
There are 8 independent parts, one for each index of `dp`. A program takes and returns all parts, laid end to end along the dimension named above; an argument that names none is the same for every part. Nothing has to cross between parts.
Inputs may be any that keep to these rules, and one draw needn't show every extreme that they name: doc_start[i] is the index of the first token of token i's document: it never falls, doc_start[i] <= i < doc_start[i] + 1024, some document has exactly 1024 tokens, and every document but the last has 128 tokens or more. `positions`: within one document the position rises by one from each token to the next.
All inputs are finite; a program needn't handle non-finite values.
Results may differ from a plain program's by a relative error of at most 0.0039.
The roundings to bfloat16 on the way count: a program that leaves them out, or rounds other values in their place, can miss the bound.
Values may be sent and summed in bfloat16 or wider, within the bound.
A program may use at most 64 MiB of HBM per device.

v0:
```python
import jax
import jax.numpy as jnp
from jax import lax
from jax.sharding import PartitionSpec as P

QUERY_HEADS = 64
KEY_VALUE_HEADS = 8
HEAD_SIZE = 128
DOC_MAX = 1024


ROPE_BASE = 1000000.0
NORM_EPS = 1e-06


def from_behind(value, axis, steps):
    count = lax.axis_size(axis)
    leading, last = (max(0, -steps), min(count, count - steps))
    return lax.ppermute(value, axis, [(source, source + steps) for source in range(leading, last)])


def rotary_tables(positions):
    half_dim = HEAD_SIZE // 2
    inv_freq = ROPE_BASE ** (-(jnp.arange(half_dim, dtype=jnp.float32) * 2.0 / HEAD_SIZE))
    angle = positions.astype(jnp.float32)[:, None] * inv_freq[None, :]
    return (jnp.cos(angle), jnp.sin(angle))


def normalize_and_rotate(heads_in, gain, cosine_table, sine_table):
    upcast = heads_in.astype(jnp.float32)
    mean_square = jnp.mean(upcast * upcast, axis=-1, keepdims=True)
    normed = upcast * lax.rsqrt(mean_square + NORM_EPS) * gain
    half_dim = normed.shape[-1] // 2
    first_half = normed[..., :half_dim]
    second_half = normed[..., half_dim:]
    cos_rows = cosine_table[:, None, :]
    sin_rows = sine_table[:, None, :]
    rotated = jnp.concatenate(
        [
            first_half * cos_rows - second_half * sin_rows,
            second_half * cos_rows + first_half * sin_rows,
        ],
        axis=-1,
    )
    return rotated.astype(jnp.bfloat16)


def window_attend(q_rope, k_window, v_window, starts, my_first, window_first):
    device_rows = q_rope.shape[0]
    window_rows = k_window.shape[0]
    head_copies = QUERY_HEADS // KEY_VALUE_HEADS
    scale = HEAD_SIZE ** (-0.5)
    q_grouped = jnp.transpose(
        q_rope.reshape(device_rows, KEY_VALUE_HEADS, head_copies, HEAD_SIZE), (1, 2, 0, 3)
    )
    q_grouped = q_grouped.reshape(KEY_VALUE_HEADS, head_copies * device_rows, HEAD_SIZE)
    k_major = jnp.transpose(k_window, (1, 0, 2))
    v_major = jnp.transpose(v_window, (1, 0, 2))
    row_index = my_first + jnp.arange(device_rows, dtype=jnp.int32)
    key_index = window_first + jnp.arange(window_rows, dtype=jnp.int32)
    visible = (key_index[None, :] >= starts[:, None]) & (key_index[None, :] <= row_index[:, None])

    def one_group(operands):
        query_rows, key_rows, value_rows = operands
        scores = jnp.dot(query_rows, key_rows.T, preferred_element_type=jnp.float32) * scale
        scores = scores.reshape(head_copies, device_rows, window_rows)
        scores = jnp.where(visible[None, :, :], scores, -jnp.inf)
        row_max = jnp.max(scores, axis=2, keepdims=True)
        exp_scores = jnp.exp(scores - row_max)
        row_total = jnp.sum(exp_scores, axis=2, keepdims=True)
        weights = exp_scores.astype(jnp.bfloat16).reshape(head_copies * device_rows, window_rows)
        mixed_out = jnp.dot(weights, value_rows, preferred_element_type=jnp.float32)
        mixed_out = mixed_out.reshape(head_copies, device_rows, HEAD_SIZE) / row_total
        return mixed_out.astype(jnp.bfloat16)

    grouped_out = lax.map(one_group, (q_grouped, k_major, v_major))
    return jnp.transpose(grouped_out, (2, 0, 1, 3)).reshape(device_rows, QUERY_HEADS * HEAD_SIZE)


def body(
    query_proj, key_projection, value_projection, query_gain, key_norm_gain, positions, doc_start
):
    device_rows = query_proj.shape[0]
    cosine_table, sine_table = rotary_tables(positions)
    q_rope = normalize_and_rotate(
        query_proj.reshape(device_rows, QUERY_HEADS, HEAD_SIZE),
        query_gain,
        cosine_table,
        sine_table,
    )
    key_rotated = normalize_and_rotate(
        key_projection.reshape(device_rows, KEY_VALUE_HEADS, HEAD_SIZE),
        key_norm_gain,
        cosine_table,
        sine_table,
    )
    value_head_split = value_projection.reshape(device_rows, KEY_VALUE_HEADS, HEAD_SIZE)
    my_first = lax.axis_index("sp") * device_rows
    reach = (DOC_MAX + device_rows - 1) // device_rows
    own_pair = jnp.stack([key_rotated, value_head_split])
    earlier = []
    for distance in range(reach, 0, -1):
        earlier.append(from_behind(own_pair, "sp", distance))
    window = jnp.concatenate(earlier + [own_pair], axis=1)
    window_first = my_first - reach * device_rows
    return window_attend(q_rope, window[0], window[1], doc_start, my_first, window_first)


def solution(mesh):
    in_specs = (
        P(("dp", "sp"), None),
        P(("dp", "sp"), None),
        P(("dp", "sp"), None),
        P(),
        P(),
        P(("dp", "sp")),
        P(("dp", "sp")),
    )
    out_specs = P(("dp", "sp"), None)
    return jax.shard_map(body, mesh=mesh, in_specs=in_specs, out_specs=out_specs, check_vma=False)
```

profile of v0, /device:TPU:80, one launch (start us, length us, event | category | flops | bytes accessed | tf_op | source)
XLA Modules:
  0.0 180.5 jit_solution(6062271254652235105)
XLA Ops:
  4.3 4.3 %collective-permute-start = (bf16[2,128,8,128]{1,3,2,0:T(8,128)(2,1)S(1)}, bf16[2,128,8,128]{1,3,2,0:T(8,128)(2,1)}, u32[]{:S(2)}, u32[]{:S(2)}) collective-permute-start(bf16[2,128,8,128]{1,3,2,0:T(8,128)(2,1)S(1)} %pad_maximum_fusion.1), channel_id=1, source_target_pairs={{0,64},{8,72},{16,80},{24,88},{32,96},{40,104},{48,112},{56,120},{... | collective-permute-start | bytes 1572872 | tf_op jit(solution)/shard_map/ppermute | solution.py:19
  8.5 3.2 %collective-permute-start.1 = (bf16[2,128,8,128]{1,3,2,0:T(8,128)(2,1)S(1)}, bf16[2,128,8,128]{1,3,2,0:T(8,128)(2,1)}, u32[]{:S(2)}, u32[]{:S(2)}) collective-permute-start(bf16[2,128,8,128]{1,3,2,0:T(8,128)(2,1)S(1)} %pad_maximum_fusion.1), channel_id=1, source_target_pairs={{0,56},{8,64},{16,72},{24,80},{32,88},{40,96},{48,104},{56,112},{6... | collective-permute-start | bytes 1572872 | tf_op jit(solution)/shard_map/ppermute | solution.py:19
  11.8 6.2 %collective-permute-start.2 = (bf16[2,128,8,128]{1,3,2,0:T(8,128)(2,1)S(1)}, bf16[2,128,8,128]{1,3,2,0:T(8,128)(2,1)}, u32[]{:S(2)}, u32[]{:S(2)}) collective-permute-start(bf16[2,128,8,128]{1,3,2,0:T(8,128)(2,1)S(1)} %pad_maximum_fusion.1), channel_id=1, source_target_pairs={{0,48},{8,56},{16,64},{24,72},{32,80},{40,88},{48,96},{56,104},{64... | collective-permute-start | bytes 1572872 | tf_op jit(solution)/shard_map/ppermute | solution.py:19
  17.9 7.3 %collective-permute-start.3 = (bf16[2,128,8,128]{1,3,2,0:T(8,128)(2,1)S(1)}, bf16[2,128,8,128]{1,3,2,0:T(8,128)(2,1)}, u32[]{:S(2)}, u32[]{:S(2)}) collective-permute-start(bf16[2,128,8,128]{1,3,2,0:T(8,128)(2,1)S(1)} %pad_maximum_fusion.1), channel_id=1, source_target_pairs={{0,40},{8,48},{16,56},{24,64},{32,72},{40,80},{48,88},{56,96},{64,... | collective-permute-start | bytes 1572872 | tf_op jit(solution)/shard_map/ppermute | solution.py:19
  25.3 2.9 %collective-permute-start.4 = (bf16[2,128,8,128]{1,3,2,0:T(8,128)(2,1)S(1)}, bf16[2,128,8,128]{1,3,2,0:T(8,128)(2,1)}, u32[]{:S(2)}, u32[]{:S(2)}) collective-permute-start(bf16[2,128,8,128]{1,3,2,0:T(8,128)(2,1)S(1)} %pad_maximum_fusion.1), channel_id=1, source_target_pairs={{0,32},{8,40},{16,48},{24,56},{32,64},{40,72},{48,80},{56,88},{64,... | collective-permute-start | bytes 1572872 | tf_op jit(solution)/shard_map/ppermute | solution.py:19
  36.6 2.5 %pad_maximum_fusion = bf16[128,8,8,128]{3,0,2,1:T(8,128)(2,1)} fusion(bf16[128,8,8,64]{3,0,2,1:T(8,128)(2,1)S(1)} %bitcast.76, bf16[128,8,8,64]{3,0,2,1:T(8,128)(2,1)S(1)} %bitcast.75), kind=kLoop, calls=%fused_computation.27 | loop fusion | flops 4194304 | bytes 4194304 | tf_op jit(solution)/shard_map/concatenate | solution.py:38
  39.1 4.9 %collective-permute-start.5 = (bf16[2,128,8,128]{1,3,2,0:T(8,128)(2,1)S(1)}, bf16[2,128,8,128]{1,3,2,0:T(8,128)(2,1)S(1)}, u32[]{:S(2)}, u32[]{:S(2)}) collective-permute-start(bf16[2,128,8,128]{1,3,2,0:T(8,128)(2,1)S(1)} %pad_maximum_fusion.1), channel_id=1, source_target_pairs={{0,24},{8,32},{16,40},{24,48},{32,56},{40,64},{48,72},{56,80},{64,... | collective-permute-start | bytes 1572872 | tf_op jit(solution)/shard_map/ppermute | solution.py:19
  45.2 4.5 %collective-permute-start.6 = (bf16[2,128,8,128]{1,3,2,0:T(8,128)(2,1)S(1)}, bf16[2,128,8,128]{1,3,2,0:T(8,128)(2,1)S(1)}, u32[]{:S(2)}, u32[]{:S(2)}) collective-permute-start(bf16[2,128,8,128]{1,3,2,0:T(8,128)(2,1)S(1)} %pad_maximum_fusion.1), channel_id=1, source_target_pairs={{0,16},{8,24},{16,32},{24,40},{32,48},{40,56},{48,64},{56,72},{64,... | collective-permute-start | bytes 1572872 | tf_op jit(solution)/shard_map/ppermute | solution.py:19
  50.8 38.3 %collective-permute-done.2 = bf16[2,128,8,128]{1,3,2,0:T(8,128)(2,1)} collective-permute-done((bf16[2,128,8,128]{1,3,2,0:T(8,128)(2,1)S(1)}, bf16[2,128,8,128]{1,3,2,0:T(8,128)(2,1)}, u32[]{:S(2)}, u32[]{:S(2)}) %collective-permute-start.2) | collective-permute-done | bytes 524320 | tf_op jit(solution)/shard_map/ppermute | solution.py:19
  89.2 2.1 %collective-permute-start.7 = (bf16[2,128,8,128]{1,3,2,0:T(8,128)(2,1)S(1)}, bf16[2,128,8,128]{1,3,2,0:T(8,128)(2,1)S(1)}, u32[]{:S(2)}, u32[]{:S(2)}) collective-permute-start(bf16[2,128,8,128]{1,3,2,0:T(8,128)(2,1)S(1)} %pad_maximum_fusion.1), channel_id=1, source_target_pairs={{0,8},{8,16},{16,24},{24,32},{32,40},{40,48},{48,56},{56,64},{64,7... | collective-permute-start | bytes 1572872 | tf_op jit(solution)/shard_map/ppermute | solution.py:19
  92.5 1.6 collective-permute-done.3
  96.6 26.9 %collective-permute-done.6 = bf16[2,128,8,128]{1,3,2,0:T(8,128)(2,1)S(1)} collective-permute-done((bf16[2,128,8,128]{1,3,2,0:T(8,128)(2,1)S(1)}, bf16[2,128,8,128]{1,3,2,0:T(8,128)(2,1)S(1)}, u32[]{:S(2)}, u32[]{:S(2)}) %collective-permute-start.6) | collective-permute-done | bytes 524320 | tf_op jit(solution)/shard_map/ppermute | solution.py:19
  125.1 1.8 slice_bitcast_fusion
  126.8 47.6 %while.11 = (s32[]{:T(128)}, bf16[8,8,128,128]{3,2,1,0:T(8,128)(2,1)}, bf16[8,1024,128]{2,1,0:T(8,128)(2,1)}, bf16[8,1152,128]{1,2,0:T(8,128)(2,1)S(1)}, bf16[8,...) while((s32[]{:T(128)}, ...), condition=%wide.region_5.6_spmd.clone, body=%wide.region_2.5_spmd.clone.sunk | while | flops 611760128 | bytes 17948252 | solution.py:76
  127.3 2.1 %fusion.29 = (f32[1024]{0:T(1024)S(1)}, f32[1024,1152]{1,0:T(8,128)S(1)}) fusion(pred[1024,1152]{1,0:T(32,128)(4,1)S(1)} %bitcast.72, bf16[8,1152,128]{1,2,0:T(8,128)(2,1)S(1)} %get-tuple-element.173, s32[]{:T(128)} %get-tuple-element.161, bf16[8,1024,128]{2,1,0:T(8,128)(2,1)} %get-tuple-element.172), kind=kOutput, calls=%fused_computation.53.clone.1 | convolution fusion | flops 305527808 | bytes 6460416 | tf_op jit(solution)/shard_map/while/body/eval_jaxpr/dot_general | solution.py:65
  130.3 2.5 %fusion.31 = bf16[8,8,128,128]{3,2,1,0:T(8,128)(2,1)} fusion(bf16[8,8,128,128]{3,2,1,0:T(8,128)(2,1)} %get-tuple-element.162, s32[]{:T(128)} %get-tuple-element.161, bf16[8,128,1152]{2,1,0:T(8,128)(2,1)S(1)} %bitcast.73, bf16[8,1152,128]{1,2,0:T(8,128)(2,1)} %get-tuple-element.174, f32[8,128]{1,0:T(8,128)S(1)} %bitcast.81), kind=kOutput, calls=%fused_computation.9.clone.1 | convolution fusion | flops 302252032 | bytes 2921472 | tf_op jit(solution)/shard_map/while/body/eval_jaxpr/dot_general | solution.py:72
  133.3 2.1 %fusion.29 = (f32[1024]{0:T(1024)S(1)}, f32[1024,1152]{1,0:T(8,128)S(1)}) fusion(pred[1024,1152]{1,0:T(32,128)(4,1)S(1)} %bitcast.72, bf16[8,1152,128]{1,2,0:T(8,128)(2,1)S(1)} %get-tuple-element.173, s32[]{:T(128)} %get-tuple-element.161, bf16[8,1024,128]{2,1,0:T(8,128)(2,1)} %get-tuple-element.172), kind=kOutput, calls=%fused_computation.53.clone.1 | convolution fusion | flops 305527808 | bytes 6460416 | tf_op jit(solution)/shard_map/while/body/eval_jaxpr/dot_general | solution.py:65
  136.3 2.5 %fusion.31 = bf16[8,8,128,128]{3,2,1,0:T(8,128)(2,1)} fusion(bf16[8,8,128,128]{3,2,1,0:T(8,128)(2,1)} %get-tuple-element.162, s32[]{:T(128)} %get-tuple-element.161, bf16[8,128,1152]{2,1,0:T(8,128)(2,1)S(1)} %bitcast.73, bf16[8,1152,128]{1,2,0:T(8,128)(2,1)} %get-tuple-element.174, f32[8,128]{1,0:T(8,128)S(1)} %bitcast.81), kind=kOutput, calls=%fused_computation.9.clone.1 | convolution fusion | flops 302252032 | bytes 2921472 | tf_op jit(solution)/shard_map/while/body/eval_jaxpr/dot_general | solution.py:72
  139.2 2.1 %fusion.29 = (f32[1024]{0:T(1024)S(1)}, f32[1024,1152]{1,0:T(8,128)S(1)}) fusion(pred[1024,1152]{1,0:T(32,128)(4,1)S(1)} %bitcast.72, bf16[8,1152,128]{1,2,0:T(8,128)(2,1)S(1)} %get-tuple-element.173, s32[]{:T(128)} %get-tuple-element.161, bf16[8,1024,128]{2,1,0:T(8,128)(2,1)} %get-tuple-element.172), kind=kOutput, calls=%fused_computation.53.clone.1 | convolution fusion | flops 305527808 | bytes 6460416 | tf_op jit(solution)/shard_map/while/body/eval_jaxpr/dot_general | solution.py:65
  142.2 2.5 %fusion.31 = bf16[8,8,128,128]{3,2,1,0:T(8,128)(2,1)} fusion(bf16[8,8,128,128]{3,2,1,0:T(8,128)(2,1)} %get-tuple-element.162, s32[]{:T(128)} %get-tuple-element.161, bf16[8,128,1152]{2,1,0:T(8,128)(2,1)S(1)} %bitcast.73, bf16[8,1152,128]{1,2,0:T(8,128)(2,1)} %get-tuple-element.174, f32[8,128]{1,0:T(8,128)S(1)} %bitcast.81), kind=kOutput, calls=%fused_computation.9.clone.1 | convolution fusion | flops 302252032 | bytes 2921472 | tf_op jit(solution)/shard_map/while/body/eval_jaxpr/dot_general | solution.py:72
  145.2 2.1 %fusion.29 = (f32[1024]{0:T(1024)S(1)}, f32[1024,1152]{1,0:T(8,128)S(1)}) fusion(pred[1024,1152]{1,0:T(32,128)(4,1)S(1)} %bitcast.72, bf16[8,1152,128]{1,2,0:T(8,128)(2,1)S(1)} %get-tuple-element.173, s32[]{:T(128)} %get-tuple-element.161, bf16[8,1024,128]{2,1,0:T(8,128)(2,1)} %get-tuple-element.172), kind=kOutput, calls=%fused_computation.53.clone.1 | convolution fusion | flops 305527808 | bytes 6460416 | tf_op jit(solution)/shard_map/while/body/eval_jaxpr/dot_general | solution.py:65
  148.2 2.5 %fusion.31 = bf16[8,8,128,128]{3,2,1,0:T(8,128)(2,1)} fusion(bf16[8,8,128,128]{3,2,1,0:T(8,128)(2,1)} %get-tuple-element.162, s32[]{:T(128)} %get-tuple-element.161, bf16[8,128,1152]{2,1,0:T(8,128)(2,1)S(1)} %bitcast.73, bf16[8,1152,128]{1,2,0:T(8,128)(2,1)} %get-tuple-element.174, f32[8,128]{1,0:T(8,128)S(1)} %bitcast.81), kind=kOutput, calls=%fused_computation.9.clone.1 | convolution fusion | flops 302252032 | bytes 2921472 | tf_op jit(solution)/shard_map/while/body/eval_jaxpr/dot_general | solution.py:72
  151.1 2.1 %fusion.29 = (f32[1024]{0:T(1024)S(1)}, f32[1024,1152]{1,0:T(8,128)S(1)}) fusion(pred[1024,1152]{1,0:T(32,128)(4,1)S(1)} %bitcast.72, bf16[8,1152,128]{1,2,0:T(8,128)(2,1)S(1)} %get-tuple-element.173, s32[]{:T(128)} %get-tuple-element.161, bf16[8,1024,128]{2,1,0:T(8,128)(2,1)} %get-tuple-element.172), kind=kOutput, calls=%fused_computation.53.clone.1 | convolution fusion | flops 305527808 | bytes 6460416 | tf_op jit(solution)/shard_map/while/body/eval_jaxpr/dot_general | solution.py:65
  154.1 2.5 %fusion.31 = bf16[8,8,128,128]{3,2,1,0:T(8,128)(2,1)} fusion(bf16[8,8,128,128]{3,2,1,0:T(8,128)(2,1)} %get-tuple-element.162, s32[]{:T(128)} %get-tuple-element.161, bf16[8,128,1152]{2,1,0:T(8,128)(2,1)S(1)} %bitcast.73, bf16[8,1152,128]{1,2,0:T(8,128)(2,1)} %get-tuple-element.174, f32[8,128]{1,0:T(8,128)S(1)} %bitcast.81), kind=kOutput, calls=%fused_computation.9.clone.1 | convolution fusion | flops 302252032 | bytes 2921472 | tf_op jit(solution)/shard_map/while/body/eval_jaxpr/dot_general | solution.py:72
  157.1 2.1 %fusion.29 = (f32[1024]{0:T(1024)S(1)}, f32[1024,1152]{1,0:T(8,128)S(1)}) fusion(pred[1024,1152]{1,0:T(32,128)(4,1)S(1)} %bitcast.72, bf16[8,1152,128]{1,2,0:T(8,128)(2,1)S(1)} %get-tuple-element.173, s32[]{:T(128)} %get-tuple-element.161, bf16[8,1024,128]{2,1,0:T(8,128)(2,1)} %get-tuple-element.172), kind=kOutput, calls=%fused_computation.53.clone.1 | convolution fusion | flops 305527808 | bytes 6460416 | tf_op jit(solution)/shard_map/while/body/eval_jaxpr/dot_general | solution.py:65
  160.0 2.5 %fusion.31 = bf16[8,8,128,128]{3,2,1,0:T(8,128)(2,1)} fusion(bf16[8,8,128,128]{3,2,1,0:T(8,128)(2,1)} %get-tuple-element.162, s32[]{:T(128)} %get-tuple-element.161, bf16[8,128,1152]{2,1,0:T(8,128)(2,1)S(1)} %bitcast.73, bf16[8,1152,128]{1,2,0:T(8,128)(2,1)} %get-tuple-element.174, f32[8,128]{1,0:T(8,128)S(1)} %bitcast.81), kind=kOutput, calls=%fused_computation.9.clone.1 | convolution fusion | flops 302252032 | bytes 2921472 | tf_op jit(solution)/shard_map/while/body/eval_jaxpr/dot_general | solution.py:72
  163.0 2.1 %fusion.29 = (f32[1024]{0:T(1024)S(1)}, f32[1024,1152]{1,0:T(8,128)S(1)}) fusion(pred[1024,1152]{1,0:T(32,128)(4,1)S(1)} %bitcast.72, bf16[8,1152,128]{1,2,0:T(8,128)(2,1)S(1)} %get-tuple-element.173, s32[]{:T(128)} %get-tuple-element.161, bf16[8,1024,128]{2,1,0:T(8,128)(2,1)} %get-tuple-element.172), kind=kOutput, calls=%fused_computation.53.clone.1 | convolution fusion | flops 305527808 | bytes 6460416 | tf_op jit(solution)/shard_map/while/body/eval_jaxpr/dot_general | solution.py:65
  166.0 2.5 %fusion.31 = bf16[8,8,128,128]{3,2,1,0:T(8,128)(2,1)} fusion(bf16[8,8,128,128]{3,2,1,0:T(8,128)(2,1)} %get-tuple-element.162, s32[]{:T(128)} %get-tuple-element.161, bf16[8,128,1152]{2,1,0:T(8,128)(2,1)S(1)} %bitcast.73, bf16[8,1152,128]{1,2,0:T(8,128)(2,1)} %get-tuple-element.174, f32[8,128]{1,0:T(8,128)S(1)} %bitcast.81), kind=kOutput, calls=%fused_computation.9.clone.1 | convolution fusion | flops 302252032 | bytes 2921472 | tf_op jit(solution)/shard_map/while/body/eval_jaxpr/dot_general | solution.py:72
  169.0 2.1 %fusion.29 = (f32[1024]{0:T(1024)S(1)}, f32[1024,1152]{1,0:T(8,128)S(1)}) fusion(pred[1024,1152]{1,0:T(32,128)(4,1)S(1)} %bitcast.72, bf16[8,1152,128]{1,2,0:T(8,128)(2,1)S(1)} %get-tuple-element.173, s32[]{:T(128)} %get-tuple-element.161, bf16[8,1024,128]{2,1,0:T(8,128)(2,1)} %get-tuple-element.172), kind=kOutput, calls=%fused_computation.53.clone.1 | convolution fusion | flops 305527808 | bytes 6460416 | tf_op jit(solution)/shard_map/while/body/eval_jaxpr/dot_general | solution.py:65
  171.9 2.5 %fusion.31 = bf16[8,8,128,128]{3,2,1,0:T(8,128)(2,1)} fusion(bf16[8,8,128,128]{3,2,1,0:T(8,128)(2,1)} %get-tuple-element.162, s32[]{:T(128)} %get-tuple-element.161, bf16[8,128,1152]{2,1,0:T(8,128)(2,1)S(1)} %bitcast.73, bf16[8,1152,128]{1,2,0:T(8,128)(2,1)} %get-tuple-element.174, f32[8,128]{1,0:T(8,128)S(1)} %bitcast.81), kind=kOutput, calls=%fused_computation.9.clone.1 | convolution fusion | flops 302252032 | bytes 2921472 | tf_op jit(solution)/shard_map/while/body/eval_jaxpr/dot_general | solution.py:72
  174.4 2.9 %copy.19 = bf16[128,8,8,128]{3,2,1,0:T(8,128)(2,1)S(1)} copy(bf16[128,8,8,128]{3,0,2,1:T(8,128)(2,1)} %bitcast.13) | data formatting | bytes 4194304 | tf_op jit(solution)/shard_map/transpose | solution.py:77
  177.3 3.1 %copy.25 = bf16[16,8,64,128]{3,1,2,0:T(8,128)(2,1)} copy(bf16[16,8,64,128]{3,2,1,0:T(8,128)(2,1)S(1)} %bitcast.77) | data formatting | bytes 4194304
  (67 shorter events, 31.3 us)
Async XLA Ops:
  0.0 28.4 %copy-start = (bf16[128,8192]{1,0:T(8,128)(2,1)S(1)}, bf16[128,8192]{1,0:T(8,128)(2,1)}, u32[]{:S(2)}) copy-start(bf16[128,8192]{1,0:T(8,128)(2,1)} %param.9) | copy-start | bytes 6291460
  4.3 34.9 %collective-permute-start = (bf16[2,128,8,128]{1,3,2,0:T(8,128)(2,1)S(1)}, bf16[2,128,8,128]{1,3,2,0:T(8,128)(2,1)}, u32[]{:S(2)}, u32[]{:S(2)}) collective-permute-start(bf16[2,128,8,128]{1,3,2,0:T(8,128)(2,1)S(1)} %pad_maximum_fusion.1), channel_id=1, source_target_pairs={{0,64},{8,72},{16,80},{24,88},{32,96},{40,104},{48,112},{56,120},{... | collective-permute-start | bytes 1572872 | tf_op jit(solution)/shard_map/ppermute | solution.py:19
  8.5 36.6 %collective-permute-start.1 = (bf16[2,128,8,128]{1,3,2,0:T(8,128)(2,1)S(1)}, bf16[2,128,8,128]{1,3,2,0:T(8,128)(2,1)}, u32[]{:S(2)}, u32[]{:S(2)}) collective-permute-start(bf16[2,128,8,128]{1,3,2,0:T(8,128)(2,1)S(1)} %pad_maximum_fusion.1), channel_id=1, source_target_pairs={{0,56},{8,64},{16,72},{24,80},{32,88},{40,96},{48,104},{56,112},{6... | collective-permute-start | bytes 1572872 | tf_op jit(solution)/shard_map/ppermute | solution.py:19
  11.8 77.4 %collective-permute-start.2 = (bf16[2,128,8,128]{1,3,2,0:T(8,128)(2,1)S(1)}, bf16[2,128,8,128]{1,3,2,0:T(8,128)(2,1)}, u32[]{:S(2)}, u32[]{:S(2)}) collective-permute-start(bf16[2,128,8,128]{1,3,2,0:T(8,128)(2,1)S(1)} %pad_maximum_fusion.1), channel_id=1, source_target_pairs={{0,48},{8,56},{16,64},{24,72},{32,80},{40,88},{48,96},{56,104},{64... | collective-permute-start | bytes 1572872 | tf_op jit(solution)/shard_map/ppermute | solution.py:19
  17.9 76.1 %collective-permute-start.3 = (bf16[2,128,8,128]{1,3,2,0:T(8,128)(2,1)S(1)}, bf16[2,128,8,128]{1,3,2,0:T(8,128)(2,1)}, u32[]{:S(2)}, u32[]{:S(2)}) collective-permute-start(bf16[2,128,8,128]{1,3,2,0:T(8,128)(2,1)S(1)} %pad_maximum_fusion.1), channel_id=1, source_target_pairs={{0,40},{8,48},{16,56},{24,64},{32,72},{40,80},{48,88},{56,96},{64,... | collective-permute-start | bytes 1572872 | tf_op jit(solution)/shard_map/ppermute | solution.py:19
  25.3 69.9 %collective-permute-start.4 = (bf16[2,128,8,128]{1,3,2,0:T(8,128)(2,1)S(1)}, bf16[2,128,8,128]{1,3,2,0:T(8,128)(2,1)}, u32[]{:S(2)}, u32[]{:S(2)}) collective-permute-start(bf16[2,128,8,128]{1,3,2,0:T(8,128)(2,1)S(1)} %pad_maximum_fusion.1), channel_id=1, source_target_pairs={{0,32},{8,40},{16,48},{24,56},{32,64},{40,72},{48,80},{56,88},{64,... | collective-permute-start | bytes 1572872 | tf_op jit(solution)/shard_map/ppermute | solution.py:19
  29.6 1.2 copy-start.2
  39.1 57.3 %collective-permute-start.5 = (bf16[2,128,8,128]{1,3,2,0:T(8,128)(2,1)S(1)}, bf16[2,128,8,128]{1,3,2,0:T(8,128)(2,1)S(1)}, u32[]{:S(2)}, u32[]{:S(2)}) collective-permute-start(bf16[2,128,8,128]{1,3,2,0:T(8,128)(2,1)S(1)} %pad_maximum_fusion.1), channel_id=1, source_target_pairs={{0,24},{8,32},{16,40},{24,48},{32,56},{40,64},{48,72},{56,80},{64,... | collective-permute-start | bytes 1572872 | tf_op jit(solution)/shard_map/ppermute | solution.py:19
  45.2 78.4 %collective-permute-start.6 = (bf16[2,128,8,128]{1,3,2,0:T(8,128)(2,1)S(1)}, bf16[2,128,8,128]{1,3,2,0:T(8,128)(2,1)S(1)}, u32[]{:S(2)}, u32[]{:S(2)}) collective-permute-start(bf16[2,128,8,128]{1,3,2,0:T(8,128)(2,1)S(1)} %pad_maximum_fusion.1), channel_id=1, source_target_pairs={{0,16},{8,24},{16,32},{24,40},{32,48},{40,56},{48,64},{56,72},{64,... | collective-permute-start | bytes 1572872 | tf_op jit(solution)/shard_map/ppermute | solution.py:19
  89.2 35.6 %collective-permute-start.7 = (bf16[2,128,8,128]{1,3,2,0:T(8,128)(2,1)S(1)}, bf16[2,128,8,128]{1,3,2,0:T(8,128)(2,1)S(1)}, u32[]{:S(2)}, u32[]{:S(2)}) collective-permute-start(bf16[2,128,8,128]{1,3,2,0:T(8,128)(2,1)S(1)} %pad_maximum_fusion.1), channel_id=1, source_target_pairs={{0,8},{8,16},{16,24},{24,32},{32,40},{40,48},{48,56},{56,64},{64,7... | collective-permute-start | bytes 1572872 | tf_op jit(solution)/shard_map/ppermute | solution.py:19
  125.1 1.8 copy-start.1
where the time goes:
time: 182 us; the launch traced here: 180 us
  waiting for transfers between devices  68 us (37%)
  matrix products  36.1 us (20%)
  starting transfers between devices  35.4 us (19%)
  local copies, waits for them, and re-layouts  22.5 us (12%)
  other arithmetic  18 us (10%)
    ppermute x8, waiting for transfers between devices, from_behind(): lax.ppermute(value, axis, [(source, source + steps) for source in range(l...  68 us
    ppermute x8, starting transfers between devices, from_behind(): lax.ppermute(value, axis, [(source, source + steps) for source in range(l...  35.4 us
    dot_general x8, matrix products, one_group(): mixed_out = jnp.dot(weights, value_rows, preferred_element_type=jnp.float32)  19.6 us
    dot_general x8, matrix products, one_group(): jnp.dot(query_rows, key_rows.T, preferred_element_type=jnp.float32) * scale  16.5 us
    unnamed x18, local copies, waits for them, and re-layouts  12.5 us
    reduce_sum x8, other arithmetic, one_group(): row_total = jnp.sum(exp_scores, axis=2, keepdims=True)  7.4 us
  transfers between devices with their start and end apart: 8, of which 4 were waited for; matrix products, arithmetic and copies ran while one was open for 9% of the time, Pallas kernels for 0%

commit v1 on v0

v1 whole, which is shorter than its diff:
```python
import functools

import jax
import jax.numpy as jnp
import numpy as np
from jax import lax
from jax.experimental import pallas as pl
from jax.experimental.pallas import tpu as pltpu
from jax.sharding import PartitionSpec as P

QUERY_HEADS = 64
GROUPS = 8
HEAD = 128
COPIES = QUERY_HEADS // GROUPS
ROWS = 128
ROPE_BASE = 1000000.0
NORM_EPS = 1e-06
COLS = 4

OWN, PREV, WEST, EAST, OPP, X_P, WEST_P, EAST_P, OPP_P, HOLD_E, HOLD_K = range(11)
WINDOW = 9
SLOTS = 11
UP, TO_E, TO_W, REL_E, REL_W, LIFT_E, LIFT_K, D_X, D_W, D_E, D_O = range(11)
KINDS = 11
MESH = pl.DeviceIdType.MESH
HEADS_AT_ONCE = 2


def kernel(
    nz,
    q_hbm,
    k_ref,
    v_hbm,
    q_gain_ref,
    k_gain_ref,
    pos_ref,
    doc_ref,
    freq_ref,
    out_hbm,
    kv,
    q_in,
    out_buf,
    bias,
    cos_tab,
    sin_tab,
    send_sem,
    recv_sem,
    q_sem,
    v_sem,
    out_sem,
):
    me = lax.axis_index("sp")
    core = lax.rem(me, 2)
    y = lax.rem(lax.div(me, 2), COLS)
    z = lax.div(me, 2 * COLS)

    def device(z_at, y_at, core_at):
        return (z_at * COLS + y_at) * 2 + core_at

    east_y = lax.rem(y + 1, COLS)
    west_y = lax.rem(y + COLS - 1, COLS)
    opp_y = lax.rem(y + 2, COLS)
    east = device(z, east_y, core)
    west = device(z, west_y, core)
    up = device(lax.rem(z + 1, nz), y, core)
    down = device(lax.rem(z + nz - 1, nz), y, core)
    partner = device(z, y, 1 - core)

    src_e = jnp.where(y == 3, PREV, OWN)
    src_w = jnp.where(y >= 2, PREV, OWN)
    dst_w = jnp.where(y == 1, HOLD_E, EAST)
    dst_rel_e = jnp.where(y == 3, HOLD_K, OPP)
    src_rel_w = jnp.where(y == 0, HOLD_E, EAST)
    src_x = jnp.where(core == 0, OWN, PREV)

    def copy(r, kind):
        src, dst, target = {
            UP: (kv.at[r, OWN], kv.at[r, PREV], up),
            TO_E: (kv.at[r, src_e], kv.at[r, WEST], east),
            TO_W: (kv.at[r, src_w], kv.at[r, dst_w], west),
            REL_E: (kv.at[r, WEST, 0], kv.at[r, dst_rel_e, 0], east),
            REL_W: (kv.at[r, src_rel_w, 1], kv.at[r, OPP, 1], west),
            LIFT_E: (kv.at[r, HOLD_E], kv.at[r, EAST], up),
            LIFT_K: (kv.at[r, HOLD_K, 0], kv.at[r, OPP, 0], up),
            D_X: (kv.at[r, src_x], kv.at[r, X_P], partner),
            D_W: (kv.at[r, WEST], kv.at[r, WEST_P], partner),
            D_E: (kv.at[r, EAST], kv.at[r, EAST_P], partner),
            D_O: (kv.at[r, OPP], kv.at[r, OPP_P], partner),
        }[kind]
        return pltpu.make_async_remote_copy(
            src_ref=src,
            dst_ref=dst,
            send_sem=send_sem.at[r, kind],
            recv_sem=recv_sem.at[r, kind],
            device_id={"sp": target},
            device_id_type=MESH,
        )

    def v_copy(g):
        return pltpu.make_async_copy(
            v_hbm.at[:, pl.ds(g * HEAD, HEAD)], kv.at[g, OWN, 1], v_sem.at[g]
        )

    def q_copy(g):
        return pltpu.make_async_copy(
            q_hbm.at[:, pl.ds(g * COPIES * HEAD, COPIES * HEAD)], q_in.at[g], q_sem.at[g]
        )

    def out_copy(g):
        return pltpu.make_async_copy(
            out_buf.at[g],
            out_hbm.at[:, pl.ds(pl.multiple_of(g * COPIES * HEAD, COPIES * HEAD), COPIES * HEAD)],
            out_sem.at[g],
        )

    barrier = pltpu.get_barrier_semaphore()
    for target in (east, west, up, down, partner):
        pl.semaphore_signal(barrier, inc=1, device_id={"sp": target}, device_id_type=MESH)
    for g in range(GROUPS):
        v_copy(g).start()
    for g in range(GROUPS):
        q_copy(g).start()

    def column(row):
        return jnp.transpose(jnp.broadcast_to(row.astype(jnp.float32), (ROWS, ROWS)))

    angle = column(pos_ref[...]) * freq_ref[...]
    lane = lax.broadcasted_iota(jnp.int32, (ROWS, HEAD), 1)
    cos_tab[...] = jnp.cos(angle)
    sine = jnp.sin(angle)
    sin_tab[...] = jnp.where(lane < HEAD // 2, -sine, sine)

    def norm_rope(block, gain):
        x = block.astype(jnp.float32)
        mean_square = jnp.mean(x * x, axis=1, keepdims=True)
        normed = x * lax.rsqrt(mean_square + NORM_EPS) * gain
        turned = pltpu.roll(normed, HEAD // 2, 1)
        return (normed * cos_tab[...] + turned * sin_tab[...]).astype(jnp.bfloat16)

    for g in range(GROUPS):
        kv[g, OWN, 0] = norm_rope(k_ref[:, g * HEAD : (g + 1) * HEAD], k_gain_ref[...])
    for g in range(GROUPS):
        v_copy(g).wait()
    pl.semaphore_wait(barrier, 5)

    @pl.loop(0, GROUPS)
    def _(r):
        copy(r, UP).start()

    def spread(r):
        copy(r, UP).wait_recv()
        copy(r, TO_E).start()
        copy(r, TO_W).start()
        copy(r, D_X).start()

    def relay(r):
        copy(r, TO_E).wait_recv()
        copy(r, REL_E).start()
        copy(r, D_W).start()
        copy(r, TO_W).wait_recv()
        copy(r, REL_W).start()

        @pl.when(y == 0)
        def _():
            copy(r, LIFT_E).start()

        @pl.when(y != 0)
        def _():
            copy(r, D_E).start()

    def gather(r):
        copy(r, REL_E).wait_recv()

        @pl.when(y == 0)
        def _():
            copy(r, LIFT_K).start()
            copy(r, LIFT_E).wait_recv()
            copy(r, D_E).start()
            copy(r, LIFT_K).wait_recv()

        copy(r, REL_W).wait_recv()
        copy(r, D_O).start()

    row_first = me * ROWS
    tokens_before = column(doc_ref[...])
    row_at = (row_first + lax.broadcasted_iota(jnp.int32, (ROWS, ROWS), 0)).astype(jnp.float32)

    def base_of(slot):
        if slot == OWN:
            return me * ROWS
        if slot == X_P:
            of_prev = device(z - 1, y, 1 - core)
            return jnp.where(core == 1, me - 1, of_prev) * ROWS
        col = {PREV: y, WEST: west_y, EAST: east_y, OPP: opp_y}[
            slot if slot < X_P else slot - X_P + PREV
        ]
        at = core if slot < X_P else 1 - core
        return device(jnp.where(col >= y, z - 1, z), col, at) * ROWS

    def attend(r):
        for kind in (D_X, D_W, D_E, D_O):
            copy(r, kind).wait_recv()
        keys = kv[r, pl.ds(0, WINDOW), 0].reshape(WINDOW * ROWS, HEAD)
        values = kv[r, pl.ds(0, WINDOW), 1].reshape(WINDOW * ROWS, HEAD)
        wide = HEADS_AT_ONCE * HEAD

        @pl.loop(0, COPIES // HEADS_AT_ONCE)
        def _(step):
            at = pl.multiple_of(step * wide, wide)
            block = q_in[r, :, pl.ds(at, wide)]
            for h in range(HEADS_AT_ONCE):
                q = norm_rope(block[:, h * HEAD : (h + 1) * HEAD], q_gain_ref[...])
                scores = lax.dot_general(
                    q, keys, (((1,), (1,)), ((), ())), preferred_element_type=jnp.float32
                )
                scores = scores * HEAD ** (-0.5) + bias[...]
                top = jnp.max(scores, axis=1, keepdims=True)
                exp_scores = jnp.exp(scores - top)
                total = jnp.sum(exp_scores, axis=1, keepdims=True)
                mixed = jnp.dot(
                    exp_scores.astype(jnp.bfloat16), values, preferred_element_type=jnp.float32
                )
                out_buf[r, :, pl.ds(pl.multiple_of(at + h * HEAD, HEAD), HEAD)] = (
                    mixed / total
                ).astype(jnp.bfloat16)

        out_copy(r).start()

    spread(0)
    spread(1)
    for slot in range(WINDOW):
        key_at = (base_of(slot) + lane).astype(jnp.float32)
        seen = (key_at >= tokens_before) & (key_at <= row_at)
        bias[:, slot * ROWS : (slot + 1) * ROWS] = jnp.where(seen, 0.0, -1e30)
    for g in range(GROUPS):
        q_copy(g).wait()

    @pl.loop(0, GROUPS + 2)
    def _(i):
        @pl.when(i < GROUPS)
        def _():
            relay(i)

        @pl.when(i + 2 < GROUPS)
        def _():
            spread(i + 2)

        @pl.when(i >= 2)
        def _():
            attend(i - 2)

        @pl.when((i >= 1) & (i <= GROUPS))
        def _():
            gather(i - 1)

    @pl.loop(0, GROUPS)
    def _(r):
        for kind in (UP, TO_E, TO_W, REL_E, REL_W, D_X, D_W, D_E, D_O):
            copy(r, kind).wait_send()

        @pl.when(y == 0)
        def _():
            copy(r, LIFT_E).wait_send()
            copy(r, LIFT_K).wait_send()

        out_copy(r).wait()


def body(query, key, value, query_gain, key_gain, positions, doc_start):
    half = np.arange(HEAD // 2, dtype=np.float32)
    inv_freq = ROPE_BASE ** (-(jnp.asarray(half) * 2.0 / HEAD))
    freq = jnp.concatenate([inv_freq, inv_freq]).reshape(1, HEAD)
    nz = lax.axis_size("sp") // (2 * COLS)
    vmem = pl.BlockSpec(memory_space=pltpu.VMEM)
    anywhere = pl.BlockSpec(memory_space=pl.ANY)
    return pl.pallas_call(
        functools.partial(kernel, nz),
        out_shape=jax.ShapeDtypeStruct((ROWS, QUERY_HEADS * HEAD), jnp.bfloat16),
        in_specs=[anywhere, vmem, anywhere, vmem, vmem, vmem, vmem, vmem],
        out_specs=anywhere,
        scratch_shapes=[
            pltpu.VMEM((GROUPS, SLOTS, 2, ROWS, HEAD), jnp.bfloat16),
            pltpu.VMEM((GROUPS, ROWS, COPIES * HEAD), jnp.bfloat16),
            pltpu.VMEM((GROUPS, ROWS, COPIES * HEAD), jnp.bfloat16),
            pltpu.VMEM((ROWS, WINDOW * ROWS), jnp.float32),
            pltpu.VMEM((ROWS, HEAD), jnp.float32),
            pltpu.VMEM((ROWS, HEAD), jnp.float32),
            pltpu.SemaphoreType.DMA((GROUPS, KINDS)),
            pltpu.SemaphoreType.DMA((GROUPS, KINDS)),
            pltpu.SemaphoreType.DMA((GROUPS,)),
            pltpu.SemaphoreType.DMA((GROUPS,)),
            pltpu.SemaphoreType.DMA((GROUPS,)),
        ],
        compiler_params=pltpu.CompilerParams(
            collective_id=0, has_side_effects=True, vmem_limit_bytes=60 * 1024 * 1024
        ),
    )(
        query,
        key,
        value,
        query_gain.reshape(1, HEAD),
        key_gain.reshape(1, HEAD),
        positions.reshape(1, ROWS),
        doc_start.reshape(1, ROWS),
        freq,
    )


def solution(mesh):
    rows = P(("dp", "sp"), None)
    line = P(("dp", "sp"))
    return jax.shard_map(
        body,
        mesh=mesh,
        in_specs=(rows, rows, rows, P(), P(), line, line),
        out_specs=rows,
        check_vma=False,
    )
```

time: 182 us -> 103 us (0.57)
  the two profiles are of different devices: /device:TPU:80 before, /device:TPU:9 now
where the time goes in v1:
time: 103 us
  Pallas kernels  98.9 us (96%)
  local copies, waits for them, and re-layouts  3.1 us (3%)
    pallas_call x1, Pallas kernels, body(): pl.pallas_call(functools.partial(kernel, nz), out_shape=jax.ShapeDtypeStr...  98.9 us
    unnamed x1, local copies, waits for them, and re-layouts  3.1 us

profile of v1, /device:TPU:9, one launch (start us, length us, event | category | flops | bytes accessed | tf_op | source)
XLA Modules:
  0.0 102.6 jit_solution(3391297805850357130)
XLA Ops:
  0.0 0.6 maximum_bitcast_fusion.freq_ref
  0.6 98.9 %shard_map.82 = bf16[128,8192]{1,0:T(8,128)(2,1)} custom-call(bf16[128,8192]{1,0:T(8,128)(2,1)} %q_hbm.1, bf16[128,1024]{1,0:T(8,128)(2,1)} %k_ref.1, bf16[128,1024]{1,0:T(8,128)(2,1)} %v_hbm.1, f32[1,128]{1,0:T(1,128)} %bitcast.6, f32[1,128]{1,0:T(1,128)} %bitcast.7, s32[1,128]{1,0:T(1,128)} %bitcast.8, s32[1,128]{1,0:T(1,128)} %bitcast.9, ...), custom_call_target="tpu_custom_call" | custom-call | tf_op jit(solution)/shard_map/pallas_call | solution.py:276
  99.5 3.1 %copy.10 = bf16[128,8192]{1,0:T(8,128)(2,1)} copy(bf16[128,8192]{1,0:T(8,128)(2,1)} %shard_map.82) | data formatting | bytes 4194304
  (1 shorter events, 0.0 us)

commit v2 on v1

--- a/solution.py
+++ b/solution.py
@@ -24,6 +24,7 @@
 KINDS = 11
 MESH = pl.DeviceIdType.MESH
 HEADS_AT_ONCE = 2
+STEPS = COPIES // HEADS_AT_ONCE
 
 
 def kernel(
@@ -168,12 +169,16 @@
         def _():
             copy(r, D_E).start()
 
-    def gather(r):
+    def gather_east(r):
         copy(r, REL_E).wait_recv()
 
         @pl.when(y == 0)
         def _():
             copy(r, LIFT_K).start()
+
+    def gather_west(r):
+        @pl.when(y == 0)
+        def _():
             copy(r, LIFT_E).wait_recv()
             copy(r, D_E).start()
             copy(r, LIFT_K).wait_recv()
@@ -197,34 +202,36 @@
         at = core if slot < X_P else 1 - core
         return device(jnp.where(col >= y, z - 1, z), col, at) * ROWS
 
-    def attend(r):
-        for kind in (D_X, D_W, D_E, D_O):
-            copy(r, kind).wait_recv()
+    def attend(r, step):
+        @pl.when(step == 0)
+        def _():
+            for kind in (D_X, D_W, D_E, D_O):
+                copy(r, kind).wait_recv()
+
         keys = kv[r, pl.ds(0, WINDOW), 0].reshape(WINDOW * ROWS, HEAD)
         values = kv[r, pl.ds(0, WINDOW), 1].reshape(WINDOW * ROWS, HEAD)
         wide = HEADS_AT_ONCE * HEAD
-
-        @pl.loop(0, COPIES // HEADS_AT_ONCE)
-        def _(step):
-            at = pl.multiple_of(step * wide, wide)
-            block = q_in[r, :, pl.ds(at, wide)]
-            for h in range(HEADS_AT_ONCE):
-                q = norm_rope(block[:, h * HEAD : (h + 1) * HEAD], q_gain_ref[...])
-                scores = lax.dot_general(
-                    q, keys, (((1,), (1,)), ((), ())), preferred_element_type=jnp.float32
-                )
-                scores = scores * HEAD ** (-0.5) + bias[...]
-                top = jnp.max(scores, axis=1, keepdims=True)
-                exp_scores = jnp.exp(scores - top)
-                total = jnp.sum(exp_scores, axis=1, keepdims=True)
-                mixed = jnp.dot(
-                    exp_scores.astype(jnp.bfloat16), values, preferred_element_type=jnp.float32
-                )
-                out_buf[r, :, pl.ds(pl.multiple_of(at + h * HEAD, HEAD), HEAD)] = (
-                    mixed / total
-                ).astype(jnp.bfloat16)
-
-        out_copy(r).start()
+        at = pl.multiple_of(step * wide, wide)
+        block = q_in[r, :, pl.ds(at, wide)]
+        for h in range(HEADS_AT_ONCE):
+            q = norm_rope(block[:, h * HEAD : (h + 1) * HEAD], q_gain_ref[...])
+            scores = lax.dot_general(
+                q, keys, (((1,), (1,)), ((), ())), preferred_element_type=jnp.float32
+            )
+            scores = scores * HEAD ** (-0.5) + bias[...]
+            top = jnp.max(scores, axis=1, keepdims=True)
+            exp_scores = jnp.exp(scores - top)
+            total = jnp.sum(exp_scores, axis=1, keepdims=True)
+            mixed = jnp.dot(
+                exp_scores.astype(jnp.bfloat16), values, preferred_element_type=jnp.float32
+            )
+            out_buf[r, :, pl.ds(pl.multiple_of(at + h * HEAD, HEAD), HEAD)] = (
+                mixed / total
+            ).astype(jnp.bfloat16)
+
+        @pl.when(step == STEPS - 1)
+        def _():
+            out_copy(r).start()
 
     spread(0)
     spread(1)
@@ -235,23 +242,30 @@
     for g in range(GROUPS):
         q_copy(g).wait()
 
-    @pl.loop(0, GROUPS + 2)
-    def _(i):
-        @pl.when(i < GROUPS)
+    @pl.loop(0, (GROUPS + 2) * STEPS)
+    def _(t):
+        i = lax.div(t, STEPS)
+        step = lax.rem(t, STEPS)
+
+        @pl.when((step == 0) & (i < GROUPS))
         def _():
             relay(i)
 
-        @pl.when(i + 2 < GROUPS)
+        @pl.when((step == 0) & (i + 2 < GROUPS))
         def _():
             spread(i + 2)
 
+        @pl.when((step == 1) & (i >= 1) & (i <= GROUPS))
+        def _():
+            gather_east(i - 1)
+
+        @pl.when((step == STEPS - 1) & (i >= 1) & (i <= GROUPS))
+        def _():
+            gather_west(i - 1)
+
         @pl.when(i >= 2)
         def _():
-            attend(i - 2)
-
-        @pl.when((i >= 1) & (i <= GROUPS))
-        def _():
-            gather(i - 1)
+            attend(i - 2, step)
 
     @pl.loop(0, GROUPS)
     def _(r):

time: 103 us -> 82.6 us (0.80)
  the two profiles are of different devices: /device:TPU:9 before, /device:TPU:1 now
where the time goes in v2:
time: 82.6 us; the launch traced here: 82.4 us
  Pallas kernels  78.7 us (95%)
  local copies, waits for them, and re-layouts  3.1 us (4%)
    pallas_call x1, Pallas kernels, body(): pl.pallas_call(functools.partial(kernel, nz), out_shape=jax.ShapeDtypeStr...  78.7 us
    unnamed x1, local copies, waits for them, and re-layouts  3.1 us

profile of v2, /device:TPU:1, one launch (start us, length us, event | category | flops | bytes accessed | tf_op | source)
XLA Modules:
  0.0 82.4 jit_solution(3170489337427929364)
XLA Ops:
  0.0 0.6 maximum_bitcast_fusion.freq_ref
  0.6 78.7 %shard_map.82 = bf16[128,8192]{1,0:T(8,128)(2,1)} custom-call(bf16[128,8192]{1,0:T(8,128)(2,1)} %q_hbm.1, bf16[128,1024]{1,0:T(8,128)(2,1)} %k_ref.1, bf16[128,1024]{1,0:T(8,128)(2,1)} %v_hbm.1, f32[1,128]{1,0:T(1,128)} %bitcast.6, f32[1,128]{1,0:T(1,128)} %bitcast.7, s32[1,128]{1,0:T(1,128)} %bitcast.8, s32[1,128]{1,0:T(1,128)} %bitcast.9, ...), custom_call_target="tpu_custom_call" | custom-call | tf_op jit(solution)/shard_map/pallas_call | solution.py:290
  79.3 3.1 %copy.10 = bf16[128,8192]{1,0:T(8,128)(2,1)} copy(bf16[128,8192]{1,0:T(8,128)(2,1)} %shard_map.82) | data formatting | bytes 4194304
  (1 shorter events, 0.0 us)

commit v3 on v1

--- a/solution.py
+++ b/solution.py
@@ -20,16 +20,21 @@
 OWN, PREV, WEST, EAST, OPP, X_P, WEST_P, EAST_P, OPP_P, HOLD_E, HOLD_K = range(11)
 WINDOW = 9
 SLOTS = 11
-UP, TO_E, TO_W, REL_E, REL_W, LIFT_E, LIFT_K, D_X, D_W, D_E, D_O = range(11)
-KINDS = 11
+(UP, TO_EK, TO_EV, TO_WK, TO_WV, REL_E, REL_W, LIFT_E, LIFT_K, D_X, D_W, D_E, D_O) = range(13)
+KINDS = 13
 MESH = pl.DeviceIdType.MESH
-HEADS_AT_ONCE = 2
+LOOK = 2
+PAIR = 2
+STEPS = COPIES // PAIR
+KEYS = WINDOW * ROWS
+CHUNK = 32
+EXP2_SCALE = HEAD**-0.5 * 1.4426950408889634
 
 
 def kernel(
     nz,
     q_hbm,
-    k_ref,
+    k_hbm,
     v_hbm,
     q_gain_ref,
     k_gain_ref,
@@ -38,15 +43,24 @@
     freq_ref,
     out_hbm,
     kv,
+    k_in,
     q_in,
+    q_rope,
     out_buf,
     bias,
     cos_tab,
     sin_tab,
+    score_a,
+    score_b,
+    weight_a,
+    weight_b,
+    total_a,
+    total_b,
     send_sem,
     recv_sem,
     q_sem,
     v_sem,
+    k_sem,
     out_sem,
 ):
     me = lax.axis_index("sp")
@@ -62,22 +76,28 @@
     opp_y = lax.rem(y + 2, COLS)
     east = device(z, east_y, core)
     west = device(z, west_y, core)
-    up = device(lax.rem(z + 1, nz), y, core)
-    down = device(lax.rem(z + nz - 1, nz), y, core)
+    up = device(jnp.minimum(z + 1, nz - 1), y, core)
+    down = device(jnp.maximum(z - 1, 0), y, core)
     partner = device(z, y, 1 - core)
 
-    src_e = jnp.where(y == 3, PREV, OWN)
-    src_w = jnp.where(y >= 2, PREV, OWN)
+    has_up = z < nz - 1
+    has_down = z > 0
+    src_e = jnp.where((y == 3) & has_down, PREV, OWN)
+    src_w = jnp.where((y >= 2) & has_down, PREV, OWN)
     dst_w = jnp.where(y == 1, HOLD_E, EAST)
     dst_rel_e = jnp.where(y == 3, HOLD_K, OPP)
     src_rel_w = jnp.where(y == 0, HOLD_E, EAST)
-    src_x = jnp.where(core == 0, OWN, PREV)
+    src_x = jnp.where((core == 1) & has_down, PREV, OWN)
+    lifts_up = (y == 0) & has_up
+    lifted = (y == 0) & has_down
 
     def copy(r, kind):
         src, dst, target = {
             UP: (kv.at[r, OWN], kv.at[r, PREV], up),
-            TO_E: (kv.at[r, src_e], kv.at[r, WEST], east),
-            TO_W: (kv.at[r, src_w], kv.at[r, dst_w], west),
+            TO_EK: (kv.at[r, src_e, 0], kv.at[r, WEST, 0], east),
+            TO_EV: (kv.at[r, src_e, 1], kv.at[r, WEST, 1], east),
+            TO_WK: (kv.at[r, src_w, 0], kv.at[r, dst_w, 0], west),
+            TO_WV: (kv.at[r, src_w, 1], kv.at[r, dst_w, 1], west),
             REL_E: (kv.at[r, WEST, 0], kv.at[r, dst_rel_e, 0], east),
             REL_W: (kv.at[r, src_rel_w, 1], kv.at[r, OPP, 1], west),
             LIFT_E: (kv.at[r, HOLD_E], kv.at[r, EAST], up),
@@ -114,8 +134,23 @@
         )
 
     barrier = pltpu.get_barrier_semaphore()
-    for target in (east, west, up, down, partner):
+
+    def greet(target):
         pl.semaphore_signal(barrier, inc=1, device_id={"sp": target}, device_id_type=MESH)
+
+    for target in (east, west, partner):
+        greet(target)
+
+    @pl.when(has_up)
+    def _():
+        greet(up)
+
+    @pl.when(has_down)
+    def _():
+        greet(down)
+
+    k_copy = pltpu.make_async_copy(k_hbm, k_in, k_sem)
+    k_copy.start()
     for g in range(GROUPS):
         v_copy(g).start()
     for g in range(GROUPS):
@@ -137,49 +172,86 @@
         turned = pltpu.roll(normed, HEAD // 2, 1)
         return (normed * cos_tab[...] + turned * sin_tab[...]).astype(jnp.bfloat16)
 
+    @pl.when(z == 0)
+    def _():
+        kv[:, PREV] = jnp.zeros((GROUPS, 2, ROWS, HEAD), jnp.bfloat16)
+
+        @pl.when(y == 0)
+        def _():
+            kv[:, EAST] = jnp.zeros((GROUPS, 2, ROWS, HEAD), jnp.bfloat16)
+            kv[:, OPP, 0] = jnp.zeros((GROUPS, ROWS, HEAD), jnp.bfloat16)
+
+    k_copy.wait()
     for g in range(GROUPS):
-        kv[g, OWN, 0] = norm_rope(k_ref[:, g * HEAD : (g + 1) * HEAD], k_gain_ref[...])
+        kv[g, OWN, 0] = norm_rope(k_in[:, g * HEAD : (g + 1) * HEAD], k_gain_ref[...])
     for g in range(GROUPS):
         v_copy(g).wait()
-    pl.semaphore_wait(barrier, 5)
-
-    @pl.loop(0, GROUPS)
-    def _(r):
-        copy(r, UP).start()
+    pl.semaphore_wait(
+        barrier, 3 + has_up.astype(jnp.int32) + has_down.astype(jnp.int32)
+    )
+
+    @pl.when(has_up)
+    def _():
+        @pl.loop(0, GROUPS)
+        def _(r):
+            copy(r, UP).start()
 
     def spread(r):
-        copy(r, UP).wait_recv()
-        copy(r, TO_E).start()
-        copy(r, TO_W).start()
-        copy(r, D_X).start()
-
-    def relay(r):
-        copy(r, TO_E).wait_recv()
+        @pl.when(has_down)
+        def _():
+            copy(r, UP).wait_recv()
+
+        for kind in (TO_EK, TO_WV, TO_EV, TO_WK, D_X):
+            copy(r, kind).start()
+
+    def relay_first(r):
+        copy(r, TO_EK).wait_recv()
         copy(r, REL_E).start()
+        copy(r, TO_WV).wait_recv()
+        copy(r, REL_W).start()
+
+    def relay_second(r):
+        copy(r, TO_EV).wait_recv()
         copy(r, D_W).start()
-        copy(r, TO_W).wait_recv()
-        copy(r, REL_W).start()
-
+        copy(r, TO_WK).wait_recv()
+
+        @pl.when(lifts_up)
+        def _():
+            copy(r, LIFT_E).start()
+
+        @pl.when(y != 0)
+        def _():
+            copy(r, D_E).start()
+
+    def gather_first(r):
         @pl.when(y == 0)
         def _():
-            copy(r, LIFT_E).start()
+            @pl.when(has_down)
+            def _():
+                copy(r, LIFT_E).wait_recv()
+
+            copy(r, D_E).start()
+
+        copy(r, REL_E).wait_recv()
+
+        @pl.when(lifts_up)
+        def _():
+            copy(r, LIFT_K).start()
+
+        copy(r, REL_W).wait_recv()
 
         @pl.when(y != 0)
         def _():
-            copy(r, D_E).start()
-
-    def gather(r):
-        copy(r, REL_E).wait_recv()
-
+            copy(r, D_O).start()
+
+    def gather_second(r):
         @pl.when(y == 0)
         def _():
-            copy(r, LIFT_K).start()
-            copy(r, LIFT_E).wait_recv()
-            copy(r, D_E).start()
-            copy(r, LIFT_K).wait_recv()
-
-        copy(r, REL_W).wait_recv()
-        copy(r, D_O).start()
+            @pl.when(has_down)
+            def _():
+                copy(r, LIFT_K).wait_recv()
+
+            copy(r, D_O).start()
 
     row_first = me * ROWS
     tokens_before = column(doc_ref[...])
@@ -197,68 +269,113 @@
         at = core if slot < X_P else 1 - core
         return device(jnp.where(col >= y, z - 1, z), col, at) * ROWS
 
-    def attend(r):
+    scores, weights, totals = (score_a, score_b), (weight_a, weight_b), (total_a, total_b)
+
+    def arrive(r):
         for kind in (D_X, D_W, D_E, D_O):
             copy(r, kind).wait_recv()
-        keys = kv[r, pl.ds(0, WINDOW), 0].reshape(WINDOW * ROWS, HEAD)
-        values = kv[r, pl.ds(0, WINDOW), 1].reshape(WINDOW * ROWS, HEAD)
-        wide = HEADS_AT_ONCE * HEAD
-
-        @pl.loop(0, COPIES // HEADS_AT_ONCE)
-        def _(step):
-            at = pl.multiple_of(step * wide, wide)
-            block = q_in[r, :, pl.ds(at, wide)]
-            for h in range(HEADS_AT_ONCE):
-                q = norm_rope(block[:, h * HEAD : (h + 1) * HEAD], q_gain_ref[...])
-                scores = lax.dot_general(
-                    q, keys, (((1,), (1,)), ((), ())), preferred_element_type=jnp.float32
-                )
-                scores = scores * HEAD ** (-0.5) + bias[...]
-                top = jnp.max(scores, axis=1, keepdims=True)
-                exp_scores = jnp.exp(scores - top)
-                total = jnp.sum(exp_scores, axis=1, keepdims=True)
-                mixed = jnp.dot(
-                    exp_scores.astype(jnp.bfloat16), values, preferred_element_type=jnp.float32
-                )
-                out_buf[r, :, pl.ds(pl.multiple_of(at + h * HEAD, HEAD), HEAD)] = (
-                    mixed / total
-                ).astype(jnp.bfloat16)
-
-        out_copy(r).start()
-
-    spread(0)
-    spread(1)
+
+    def score(r, step):
+        keys = kv[r, pl.ds(0, WINDOW), 0].reshape(KEYS, HEAD)
+        scores[step % 2][...] = lax.dot_general(
+            q_rope[r, step], keys, (((1,), (1,)), ((), ())), preferred_element_type=jnp.float32
+        )
+
+    def weigh(step):
+        for first in range(0, PAIR * ROWS, CHUNK):
+            rows, at = pl.ds(first, CHUNK), first % ROWS
+            part = scores[step % 2][rows, :] * EXP2_SCALE + bias[at : at + CHUNK, :]
+            part = jnp.exp2(part - jnp.max(part, axis=1, keepdims=True))
+            weights[step % 2][rows, :] = part.astype(jnp.bfloat16)
+            total = part[:, :ROWS]
+            for slot in range(1, WINDOW):
+                total = total + part[:, slot * ROWS : (slot + 1) * ROWS]
+            totals[step % 2][rows, :] = total
+
+    def mix(r, step):
+        values = kv[r, pl.ds(0, WINDOW), 1].reshape(KEYS, HEAD)
+        mixed = jnp.dot(weights[step % 2][...], values, preferred_element_type=jnp.float32)
+        mixed = mixed * (1.0 / jnp.sum(totals[step % 2][...], axis=1, keepdims=True))
+        for h in range(PAIR):
+            at = (step * PAIR + h) * HEAD
+            out_buf[r, :, at : at + HEAD] = mixed[h * ROWS : (h + 1) * ROWS].astype(jnp.bfloat16)
+
+    for r in range(LOOK):
+        spread(r)
     for slot in range(WINDOW):
         key_at = (base_of(slot) + lane).astype(jnp.float32)
         seen = (key_at >= tokens_before) & (key_at <= row_at)
         bias[:, slot * ROWS : (slot + 1) * ROWS] = jnp.where(seen, 0.0, -1e30)
-    for g in range(GROUPS):
+
+    @pl.loop(0, GROUPS)
+    def _(g):
         q_copy(g).wait()
+        for h in range(COPIES):
+            q_rope[g, h // PAIR, (h % PAIR) * ROWS : (h % PAIR + 1) * ROWS] = norm_rope(
+                q_in[g, :, h * HEAD : (h + 1) * HEAD], q_gain_ref[...]
+            )
 
     @pl.loop(0, GROUPS + 2)
     def _(i):
-        @pl.when(i < GROUPS)
-        def _():
-            relay(i)
-
-        @pl.when(i + 2 < GROUPS)
-        def _():
-            spread(i + 2)
-
-        @pl.when(i >= 2)
-        def _():
-            attend(i - 2)
-
-        @pl.when((i >= 1) & (i <= GROUPS))
-        def _():
-            gather(i - 1)
+        def at_step(step):
+            if step == 0:
+
+                @pl.when(i < GROUPS)
+                def _():
+                    relay_first(i)
+
+                @pl.when(i + LOOK < GROUPS)
+                def _():
+                    spread(i + LOOK)
+
+                @pl.when(i >= 2)
+                def _():
+                    gather_second(i - 2)
+
+                @pl.when(i < GROUPS)
+                def _():
+                    relay_second(i)
+
+                @pl.when(i >= 2)
+                def _():
+                    arrive(i - 2)
+
+            if step == 2:
+
+                @pl.when((i >= 1) & (i <= GROUPS))
+                def _():
+                    gather_first(i - 1)
+
+        for step in range(STEPS):
+            at_step(step)
+
+            @pl.when(i >= 2)
+            def _():
+                score(i - 2, step)
+                weigh(step - 1)
+                late = jnp.maximum(i - 3, 0) if step < 2 else i - 2
+                mix(late, (step - 2) % STEPS)
+                if step == 1:
+
+                    @pl.when(i >= 3)
+                    def _():
+                        out_copy(i - 3).start()
+
+    weigh(STEPS - 1)
+    mix(GROUPS - 1, STEPS - 2)
+    mix(GROUPS - 1, STEPS - 1)
+    out_copy(GROUPS - 1).start()
 
     @pl.loop(0, GROUPS)
     def _(r):
-        for kind in (UP, TO_E, TO_W, REL_E, REL_W, D_X, D_W, D_E, D_O):
+        for kind in (TO_EK, TO_EV, TO_WK, TO_WV, REL_E, REL_W, D_X, D_W, D_E, D_O):
             copy(r, kind).wait_send()
 
-        @pl.when(y == 0)
+        @pl.when(has_up)
+        def _():
+            copy(r, UP).wait_send()
+
+        @pl.when(lifts_up)
         def _():
             copy(r, LIFT_E).wait_send()
             copy(r, LIFT_K).wait_send()
@@ -276,19 +393,28 @@
     return pl.pallas_call(
         functools.partial(kernel, nz),
         out_shape=jax.ShapeDtypeStruct((ROWS, QUERY_HEADS * HEAD), jnp.bfloat16),
-        in_specs=[anywhere, vmem, anywhere, vmem, vmem, vmem, vmem, vmem],
+        in_specs=[anywhere, anywhere, anywhere, vmem, vmem, vmem, vmem, vmem],
         out_specs=anywhere,
         scratch_shapes=[
             pltpu.VMEM((GROUPS, SLOTS, 2, ROWS, HEAD), jnp.bfloat16),
+            pltpu.VMEM((ROWS, GROUPS * HEAD), jnp.bfloat16),
             pltpu.VMEM((GROUPS, ROWS, COPIES * HEAD), jnp.bfloat16),
+            pltpu.VMEM((GROUPS, STEPS, PAIR * ROWS, HEAD), jnp.bfloat16),
             pltpu.VMEM((GROUPS, ROWS, COPIES * HEAD), jnp.bfloat16),
-            pltpu.VMEM((ROWS, WINDOW * ROWS), jnp.float32),
+            pltpu.VMEM((ROWS, KEYS), jnp.float32),
             pltpu.VMEM((ROWS, HEAD), jnp.float32),
             pltpu.VMEM((ROWS, HEAD), jnp.float32),
+            pltpu.VMEM((PAIR * ROWS, KEYS), jnp.float32),
+            pltpu.VMEM((PAIR * ROWS, KEYS), jnp.float32),
+            pltpu.VMEM((PAIR * ROWS, KEYS), jnp.bfloat16),
+            pltpu.VMEM((PAIR * ROWS, KEYS), jnp.bfloat16),
+            pltpu.VMEM((PAIR * ROWS, ROWS), jnp.float32),
+            pltpu.VMEM((PAIR * ROWS, ROWS), jnp.float32),
             pltpu.SemaphoreType.DMA((GROUPS, KINDS)),
             pltpu.SemaphoreType.DMA((GROUPS, KINDS)),
             pltpu.SemaphoreType.DMA((GROUPS,)),
             pltpu.SemaphoreType.DMA((GROUPS,)),
+            pltpu.SemaphoreType.DMA,
             pltpu.SemaphoreType.DMA((GROUPS,)),
         ],
         compiler_params=pltpu.CompilerParams(

time: 103 us -> 67.6 us (0.66)
  the two profiles are of different devices: /device:TPU:9 before, /device:TPU:453 now
where the time goes in v3:
time: 67.6 us; the launch traced here: 67.5 us
  Pallas kernels  63.8 us (94%)
  local copies, waits for them, and re-layouts  3.1 us (5%)
    pallas_call x1, Pallas kernels, body(): pl.pallas_call(functools.partial(kernel, nz), out_shape=jax.ShapeDtypeStr...  63.8 us
    unnamed x1, local copies, waits for them, and re-layouts  3.1 us

profile of v3, /device:TPU:453, one launch (start us, length us, event | category | flops | bytes accessed | tf_op | source)
XLA Modules:
  0.0 67.5 jit_solution(4284124780273520590)
XLA Ops:
  0.0 0.6 maximum_bitcast_fusion.freq_ref
  0.6 63.8 %shard_map.82 = bf16[128,8192]{1,0:T(8,128)(2,1)} custom-call(bf16[128,8192]{1,0:T(8,128)(2,1)} %q_hbm.1, bf16[128,1024]{1,0:T(8,128)(2,1)} %k_hbm.1, bf16[128,1024]{1,0:T(8,128)(2,1)} %v_hbm.1, f32[1,128]{1,0:T(1,128)} %bitcast.6, f32[1,128]{1,0:T(1,128)} %bitcast.7, s32[1,128]{1,0:T(1,128)} %bitcast.8, s32[1,128]{1,0:T(1,128)} %bitcast.9, ...), custom_call_target="tpu_custom_call" | custom-call | tf_op jit(solution)/shard_map/pallas_call | solution.py:393
  64.4 3.1 %copy.10 = bf16[128,8192]{1,0:T(8,128)(2,1)} copy(bf16[128,8192]{1,0:T(8,128)(2,1)} %shard_map.82) | data formatting | bytes 4194304
  (1 shorter events, 0.0 us)

commit v4 on v3

--- a/solution.py
+++ b/solution.py
@@ -28,6 +28,7 @@
 STEPS = COPIES // PAIR
 KEYS = WINDOW * ROWS
 CHUNK = 32
+FAR = 2.0**20
 EXP2_SCALE = HEAD**-0.5 * 1.4426950408889634
 
 
@@ -41,28 +42,20 @@
     pos_ref,
     doc_ref,
     freq_ref,
-    out_hbm,
+    out_ref,
     kv,
     k_in,
     q_in,
     q_rope,
-    out_buf,
     bias,
     cos_tab,
     sin_tab,
-    score_a,
-    score_b,
-    weight_a,
-    weight_b,
-    total_a,
-    total_b,
-    send_sem,
-    recv_sem,
-    q_sem,
-    v_sem,
-    k_sem,
-    out_sem,
+    q_mask,
+    k_mask,
+    *rest,
 ):
+    scores, tops, weights, totals = (rest[4 * n : 4 * n + 4] for n in range(4))
+    send_sem, recv_sem, q_sem, v_sem, k_sem = rest[16:]
     me = lax.axis_index("sp")
     core = lax.rem(me, 2)
     y = lax.rem(lax.div(me, 2), COLS)
@@ -123,14 +116,7 @@
 
     def q_copy(g):
         return pltpu.make_async_copy(
-            q_hbm.at[:, pl.ds(g * COPIES * HEAD, COPIES * HEAD)], q_in.at[g], q_sem.at[g]
-        )
-
-    def out_copy(g):
-        return pltpu.make_async_copy(
-            out_buf.at[g],
-            out_hbm.at[:, pl.ds(pl.multiple_of(g * COPIES * HEAD, COPIES * HEAD), COPIES * HEAD)],
-            out_sem.at[g],
+            q_hbm.at[:, pl.ds(pl.multiple_of(g * COPIES * HEAD, COPIES * HEAD), COPIES * HEAD)], q_in.at[g], q_sem.at[g]
         )
 
     barrier = pltpu.get_barrier_semaphore()
@@ -192,17 +178,39 @@
 
     @pl.when(has_up)
     def _():
-        @pl.loop(0, GROUPS)
+        @pl.loop(0, jnp.where(y == 0, LOOK, GROUPS))
         def _(r):
             copy(r, UP).start()
 
-    def spread(r):
-        @pl.when(has_down)
-        def _():
-            copy(r, UP).wait_recv()
-
-        for kind in (TO_EK, TO_WV, TO_EV, TO_WK, D_X):
-            copy(r, kind).start()
+    def spread_own(r):
+        @pl.when((z == 0) | (y < 3))
+        def _():
+            copy(r, TO_EK).start()
+            copy(r, TO_EV).start()
+
+        @pl.when((z == 0) | (y < 2))
+        def _():
+            copy(r, TO_WV).start()
+            copy(r, TO_WK).start()
+
+    def spread_above(r):
+        @pl.when(y != 0)
+        def _():
+            @pl.when(has_down)
+            def _():
+                copy(r, UP).wait_recv()
+
+                @pl.when(y == 3)
+                def _():
+                    copy(r, TO_EK).start()
+                    copy(r, TO_EV).start()
+
+                @pl.when(y >= 2)
+                def _():
+                    copy(r, TO_WV).start()
+                    copy(r, TO_WK).start()
+
+            copy(r, D_X).start()
 
     def relay_first(r):
         copy(r, TO_EK).wait_recv()
@@ -224,25 +232,35 @@
             copy(r, D_E).start()
 
     def gather_first(r):
+        copy(r, REL_E).wait_recv()
+
+        @pl.when(lifts_up)
+        def _():
+            copy(r, LIFT_K).start()
+
+            @pl.when(r + LOOK < GROUPS)
+            def _():
+                copy(r + LOOK, UP).start()
+
+        copy(r, REL_W).wait_recv()
+
+        @pl.when(y != 0)
+        def _():
+            copy(r, D_O).start()
+
         @pl.when(y == 0)
         def _():
             @pl.when(has_down)
             def _():
+                copy(r, UP).wait_recv()
+
+            copy(r, D_X).start()
+
+            @pl.when(has_down)
+            def _():
                 copy(r, LIFT_E).wait_recv()
 
             copy(r, D_E).start()
-
-        copy(r, REL_E).wait_recv()
-
-        @pl.when(lifts_up)
-        def _():
-            copy(r, LIFT_K).start()
-
-        copy(r, REL_W).wait_recv()
-
-        @pl.when(y != 0)
-        def _():
-            copy(r, D_O).start()
 
     def gather_second(r):
         @pl.when(y == 0)
@@ -252,6 +270,21 @@
                 copy(r, LIFT_K).wait_recv()
 
             copy(r, D_O).start()
+
+    def finish_sends():
+        @pl.loop(0, GROUPS)
+        def _(r):
+            for kind in (TO_EK, TO_EV, TO_WK, TO_WV, REL_E, REL_W, D_X, D_W, D_E, D_O):
+                copy(r, kind).wait_send()
+
+            @pl.when(has_up)
+            def _():
+                copy(r, UP).wait_send()
+
+            @pl.when(lifts_up)
+            def _():
+                copy(r, LIFT_E).wait_send()
+                copy(r, LIFT_K).wait_send()
 
     row_first = me * ROWS
     tokens_before = column(doc_ref[...])
@@ -269,118 +302,148 @@
         at = core if slot < X_P else 1 - core
         return device(jnp.where(col >= y, z - 1, z), col, at) * ROWS
 
-    scores, weights, totals = (score_a, score_b), (weight_a, weight_b), (total_a, total_b)
-
     def arrive(r):
         for kind in (D_X, D_W, D_E, D_O):
             copy(r, kind).wait_recv()
 
     def score(r, step):
         keys = kv[r, pl.ds(0, WINDOW), 0].reshape(KEYS, HEAD)
-        scores[step % 2][...] = lax.dot_general(
-            q_rope[r, step], keys, (((1,), (1,)), ((), ())), preferred_element_type=jnp.float32
+        scores[step][...] = lax.dot_general(
+            jnp.concatenate([q_rope[r, step], q_mask[...]], axis=1),
+            jnp.concatenate([keys, k_mask[...]], axis=1),
+            (((1,), (1,)), ((), ())),
+            preferred_element_type=jnp.float32,
         )
 
+    def chunks():
+        for first in range(0, PAIR * ROWS, CHUNK):
+            yield pl.ds(first, CHUNK), pl.ds(first % ROWS, CHUNK)
+
+    def peak(step):
+        for rows, own in chunks():
+            top = scores[step][rows, :ROWS] + bias[own, :]
+            for slot in range(1, WINDOW):
+                top = jnp.maximum(top, scores[step][rows, slot * ROWS : (slot + 1) * ROWS])
+            top = jnp.max(top, axis=1, keepdims=True) * EXP2_SCALE
+            tops[step][rows, :] = jnp.broadcast_to(top, (CHUNK, ROWS))
+
     def weigh(step):
-        for first in range(0, PAIR * ROWS, CHUNK):
-            rows, at = pl.ds(first, CHUNK), first % ROWS
-            part = scores[step % 2][rows, :] * EXP2_SCALE + bias[at : at + CHUNK, :]
-            part = jnp.exp2(part - jnp.max(part, axis=1, keepdims=True))
-            weights[step % 2][rows, :] = part.astype(jnp.bfloat16)
-            total = part[:, :ROWS]
-            for slot in range(1, WINDOW):
-                total = total + part[:, slot * ROWS : (slot + 1) * ROWS]
-            totals[step % 2][rows, :] = total
+        for rows, own in chunks():
+            top = tops[step][rows, :]
+            total = None
+            for slot in range(WINDOW):
+                at = slice(slot * ROWS, (slot + 1) * ROWS)
+                part = scores[step][rows, at]
+                if slot == OWN:
+                    part = part + bias[own, :]
+                part = jnp.exp2(part * EXP2_SCALE - top)
+                weights[step][rows, at] = part.astype(jnp.bfloat16)
+                total = part if total is None else total + part
+            totals[step][rows, :] = total
 
     def mix(r, step):
         values = kv[r, pl.ds(0, WINDOW), 1].reshape(KEYS, HEAD)
-        mixed = jnp.dot(weights[step % 2][...], values, preferred_element_type=jnp.float32)
-        mixed = mixed * (1.0 / jnp.sum(totals[step % 2][...], axis=1, keepdims=True))
+        mixed = jnp.dot(weights[step][...], values, preferred_element_type=jnp.float32)
+        mixed = mixed * (1.0 / jnp.sum(totals[step][...], axis=1, keepdims=True))
         for h in range(PAIR):
-            at = (step * PAIR + h) * HEAD
-            out_buf[r, :, at : at + HEAD] = mixed[h * ROWS : (h + 1) * ROWS].astype(jnp.bfloat16)
+            at = pl.multiple_of(r * COPIES * HEAD + (step * PAIR + h) * HEAD, HEAD)
+            out_ref[:, pl.ds(at, HEAD)] = mixed[h * ROWS : (h + 1) * ROWS].astype(jnp.bfloat16)
 
     for r in range(LOOK):
-        spread(r)
-    for slot in range(WINDOW):
-        key_at = (base_of(slot) + lane).astype(jnp.float32)
-        seen = (key_at >= tokens_before) & (key_at <= row_at)
-        bias[:, slot * ROWS : (slot + 1) * ROWS] = jnp.where(seen, 0.0, -1e30)
-
-    @pl.loop(0, GROUPS)
-    def _(g):
+        spread_own(r)
+    key_row = lax.broadcasted_iota(jnp.int32, (ROWS, ROWS), 0)
+    own_key = (row_first + lane).astype(jnp.float32)
+    bias[...] = jnp.where((own_key >= tokens_before) & (own_key <= row_at), 0.0, -1e30)
+    starts_here = jnp.where(tokens_before >= row_first.astype(jnp.float32), 1.0, 0.0)
+    row_flags = jnp.where(lane == 0, 1.0, jnp.where(lane == 1, starts_here, 0.0))
+    for h in range(PAIR):
+        q_mask[h * ROWS : (h + 1) * ROWS] = row_flags.astype(jnp.bfloat16)
+    k_mask[:ROWS] = jnp.zeros((ROWS, HEAD), jnp.bfloat16)
+    for slot in range(1, WINDOW):
+        key_at = (base_of(slot) + key_row).astype(jnp.float32)
+        gone = jnp.where(key_at < tokens_before[:1], -FAR, 0.0)
+        flags = jnp.where(lane == 0, gone, jnp.where(lane == 1, -FAR, 0.0))
+        k_mask[slot * ROWS : (slot + 1) * ROWS] = flags.astype(jnp.bfloat16)
+
+    def rope(g):
         q_copy(g).wait()
         for h in range(COPIES):
             q_rope[g, h // PAIR, (h % PAIR) * ROWS : (h % PAIR + 1) * ROWS] = norm_rope(
                 q_in[g, :, h * HEAD : (h + 1) * HEAD], q_gain_ref[...]
             )
 
+    @pl.loop(0, GROUPS // 2)
+    def _(g):
+        rope(g)
+
+        @pl.when(g >= GROUPS // 2 - LOOK)
+        def _():
+            spread_above(g - (GROUPS // 2 - LOOK))
+
+    def attend(r_score, step, r_mix):
+        score(r_score, step)
+        peak((step - 1) % STEPS)
+        weigh((step - 2) % STEPS)
+        mix(r_mix, (step - 3) % STEPS)
+
     @pl.loop(0, GROUPS + 2)
     def _(i):
-        def at_step(step):
-            if step == 0:
-
-                @pl.when(i < GROUPS)
-                def _():
-                    relay_first(i)
-
-                @pl.when(i + LOOK < GROUPS)
-                def _():
-                    spread(i + LOOK)
-
-                @pl.when(i >= 2)
-                def _():
-                    gather_second(i - 2)
-
-                @pl.when(i < GROUPS)
-                def _():
-                    relay_second(i)
-
-                @pl.when(i >= 2)
-                def _():
-                    arrive(i - 2)
-
-            if step == 2:
-
-                @pl.when((i >= 1) & (i <= GROUPS))
-                def _():
-                    gather_first(i - 1)
-
-        for step in range(STEPS):
-            at_step(step)
-
-            @pl.when(i >= 2)
-            def _():
-                score(i - 2, step)
-                weigh(step - 1)
-                late = jnp.maximum(i - 3, 0) if step < 2 else i - 2
-                mix(late, (step - 2) % STEPS)
-                if step == 1:
-
-                    @pl.when(i >= 3)
-                    def _():
-                        out_copy(i - 3).start()
-
-    weigh(STEPS - 1)
-    mix(GROUPS - 1, STEPS - 2)
-    mix(GROUPS - 1, STEPS - 1)
-    out_copy(GROUPS - 1).start()
-
-    @pl.loop(0, GROUPS)
-    def _(r):
-        for kind in (TO_EK, TO_EV, TO_WK, TO_WV, REL_E, REL_W, D_X, D_W, D_E, D_O):
-            copy(r, kind).wait_send()
-
-        @pl.when(has_up)
-        def _():
-            copy(r, UP).wait_send()
-
-        @pl.when(lifts_up)
-        def _():
-            copy(r, LIFT_E).wait_send()
-            copy(r, LIFT_K).wait_send()
-
-        out_copy(r).wait()
+        before = jnp.maximum(i - 3, 0)
+
+        @pl.when(i < GROUPS)
+        def _():
+            relay_first(i)
+
+        @pl.when(i + LOOK < GROUPS)
+        def _():
+            spread_own(i + LOOK)
+            spread_above(i + LOOK)
+
+        @pl.when(i < 2)
+        def _():
+            @pl.loop(0, 2)
+            def _(n):
+                rope(GROUPS // 2 + 2 * i + n)
+
+        @pl.when(i >= 3)
+        def _():
+            attend(before, 2, jnp.maximum(i - 4, 0))
+
+        @pl.when(i < GROUPS)
+        def _():
+            relay_second(i)
+
+        @pl.when(i >= 3)
+        def _():
+            attend(before, 3, before)
+
+        @pl.when((i >= 1) & (i <= GROUPS))
+        def _():
+            gather_first(i - 1)
+
+        @pl.when(i >= 2)
+        def _():
+            gather_second(i - 2)
+
+        @pl.when(i == GROUPS + 1)
+        def _():
+            finish_sends()
+
+        @pl.when(i >= 2)
+        def _():
+            arrive(i - 2)
+            attend(i - 2, 0, before)
+            attend(i - 2, 1, before)
+
+    last = GROUPS - 1
+    attend(last, 2, last - 1)
+    attend(last, 3, last)
+    peak(3)
+    weigh(2)
+    mix(last, 1)
+    weigh(3)
+    mix(last, 2)
+    mix(last, 3)
 
 
 def body(query, key, value, query_gain, key_gain, positions, doc_start):
@@ -389,33 +452,31 @@
     freq = jnp.concatenate([inv_freq, inv_freq]).reshape(1, HEAD)
     nz = lax.axis_size("sp") // (2 * COLS)
     vmem = pl.BlockSpec(memory_space=pltpu.VMEM)
-    anywhere = pl.BlockSpec(memory_space=pl.ANY)
+    anywhere = pl.BlockSpec(memory_space=pltpu.HBM)
     return pl.pallas_call(
         functools.partial(kernel, nz),
-        out_shape=jax.ShapeDtypeStruct((ROWS, QUERY_HEADS * HEAD), jnp.bfloat16),
+        out_shape=pltpu.VMEM((ROWS, QUERY_HEADS * HEAD), jnp.bfloat16),
         in_specs=[anywhere, anywhere, anywhere, vmem, vmem, vmem, vmem, vmem],
-        out_specs=anywhere,
+        out_specs=vmem,
         scratch_shapes=[
             pltpu.VMEM((GROUPS, SLOTS, 2, ROWS, HEAD), jnp.bfloat16),
             pltpu.VMEM((ROWS, GROUPS * HEAD), jnp.bfloat16),
             pltpu.VMEM((GROUPS, ROWS, COPIES * HEAD), jnp.bfloat16),
             pltpu.VMEM((GROUPS, STEPS, PAIR * ROWS, HEAD), jnp.bfloat16),
-            pltpu.VMEM((GROUPS, ROWS, COPIES * HEAD), jnp.bfloat16),
-            pltpu.VMEM((ROWS, KEYS), jnp.float32),
+            pltpu.VMEM((ROWS, ROWS), jnp.float32),
             pltpu.VMEM((ROWS, HEAD), jnp.float32),
             pltpu.VMEM((ROWS, HEAD), jnp.float32),
-            pltpu.VMEM((PAIR * ROWS, KEYS), jnp.float32),
-            pltpu.VMEM((PAIR * ROWS, KEYS), jnp.float32),
-            pltpu.VMEM((PAIR * ROWS, KEYS), jnp.bfloat16),
-            pltpu.VMEM((PAIR * ROWS, KEYS), jnp.bfloat16),
-            pltpu.VMEM((PAIR * ROWS, ROWS), jnp.float32),
-            pltpu.VMEM((PAIR * ROWS, ROWS), jnp.float32),
+            pltpu.VMEM((PAIR * ROWS, HEAD), jnp.bfloat16),
+            pltpu.VMEM((KEYS, HEAD), jnp.bfloat16),
+            *[pltpu.VMEM((PAIR * ROWS, KEYS), jnp.float32)] * STEPS,
+            *[pltpu.VMEM((PAIR * ROWS, ROWS), jnp.float32)] * STEPS,
+            *[pltpu.VMEM((PAIR * ROWS, KEYS), jnp.bfloat16)] * STEPS,
+            *[pltpu.VMEM((PAIR * ROWS, ROWS), jnp.float32)] * STEPS,
             pltpu.SemaphoreType.DMA((GROUPS, KINDS)),
             pltpu.SemaphoreType.DMA((GROUPS, KINDS)),
             pltpu.SemaphoreType.DMA((GROUPS,)),
             pltpu.SemaphoreType.DMA((GROUPS,)),
             pltpu.SemaphoreType.DMA,
-            pltpu.SemaphoreType.DMA((GROUPS,)),
         ],
         compiler_params=pltpu.CompilerParams(
             collective_id=0, has_side_effects=True, vmem_limit_bytes=60 * 1024 * 1024

time: 67.6 us -> 63.2 us (0.935)
  the two profiles are of different devices: /device:TPU:453 before, /device:TPU:193 now
where the time goes in v4:
time: 63.2 us; the launch traced here: 63.1 us
  Pallas kernels  61.1 us (97%)
  local copies, waits for them, and re-layouts  1.32 us (2%)
    pallas_call x1, Pallas kernels, body(): pl.pallas_call(functools.partial(kernel, nz), out_shape=pltpu.VMEM((ROWS,...  61.1 us
    unnamed x1, local copies, waits for them, and re-layouts  1.32 us

profile of v4, /device:TPU:193, one launch (start us, length us, event | category | flops | bytes accessed | tf_op | source)
XLA Modules:
  0.0 63.1 jit_solution(12088004111142986477)
XLA Ops:
  0.0 0.6 maximum_bitcast_fusion.freq_ref
  0.6 61.1 %shard_map.82 = bf16[128,8192]{1,0:T(8,128)(2,1)S(1)} custom-call(bf16[128,8192]{1,0:T(8,128)(2,1)} %q_hbm.1, bf16[128,1024]{1,0:T(8,128)(2,1)} %k_hbm.1, bf16[128,1024]{1,0:T(8,128)(2,1)} %v_hbm.1, f32[1,128]{1,0:T(1,128)} %bitcast.6, f32[1,128]{1,0:T(1,128)} %bitcast.7, s32[1,128]{1,0:T(1,128)} %bitcast.8, s32[1,128]{1,0:T(1,128)} %bitcast.9, ...), custom_call_target="tpu_custom_call" | custom-call | tf_op jit(solution)/shard_map/pallas_call | solution.py:456
  61.7 1.3 %copy.10 = bf16[128,8192]{1,0:T(8,128)(2,1)} copy(bf16[128,8192]{1,0:T(8,128)(2,1)S(1)} %shard_map.82) | data formatting | bytes 4194304
  (1 shorter events, 0.0 us)

commit v5 on v4

--- a/solution.py
+++ b/solution.py
@@ -386,13 +386,12 @@
         weigh((step - 2) % STEPS)
         mix(r_mix, (step - 3) % STEPS)
 
-    @pl.loop(0, GROUPS + 2)
+    last = GROUPS - 1
+
+    @pl.loop(0, GROUPS)
     def _(i):
         before = jnp.maximum(i - 3, 0)
-
-        @pl.when(i < GROUPS)
-        def _():
-            relay_first(i)
+        relay_first(i)
 
         @pl.when(i + LOOK < GROUPS)
         def _():
@@ -409,47 +408,55 @@
         def _():
             attend(before, 2, jnp.maximum(i - 4, 0))
 
-        @pl.when(i < GROUPS)
-        def _():
-            relay_second(i)
+        relay_second(i)
 
         @pl.when(i >= 3)
         def _():
             attend(before, 3, before)
 
-        @pl.when((i >= 1) & (i <= GROUPS))
+        @pl.when(i >= 1)
         def _():
             gather_first(i - 1)
 
         @pl.when(i >= 2)
         def _():
             gather_second(i - 2)
-
-        @pl.when(i == GROUPS + 1)
-        def _():
-            finish_sends()
-
-        @pl.when(i >= 2)
-        def _():
             arrive(i - 2)
             attend(i - 2, 0, before)
             attend(i - 2, 1, before)
 
-    last = GROUPS - 1
-    attend(last, 2, last - 1)
-    attend(last, 3, last)
+    attend(last - 2, 2, last - 3)
+    attend(last - 2, 3, last - 2)
+    gather_second(last - 1)
+    arrive(last - 1)
+    attend(last - 1, 0, last - 2)
+    attend(last - 1, 1, last - 2)
+    gather_first(last)
+    attend(last - 1, 2, last - 2)
+    attend(last - 1, 3, last - 1)
     peak(3)
     weigh(2)
-    mix(last, 1)
+    mix(last - 1, 1)
     weigh(3)
-    mix(last, 2)
-    mix(last, 3)
+    mix(last - 1, 2)
+    mix(last - 1, 3)
+    gather_second(last)
+    finish_sends()
+    arrive(last)
+    for step in range(STEPS + 3):
+        if step < STEPS:
+            score(last, step)
+        if 1 <= step < STEPS + 1:
+            peak(step - 1)
+        if 2 <= step < STEPS + 2:
+            weigh(step - 2)
+        if step >= 3:
+            mix(last, step - 3)
 
 
 def body(query, key, value, query_gain, key_gain, positions, doc_start):
-    half = np.arange(HEAD // 2, dtype=np.float32)
-    inv_freq = ROPE_BASE ** (-(jnp.asarray(half) * 2.0 / HEAD))
-    freq = jnp.concatenate([inv_freq, inv_freq]).reshape(1, HEAD)
+    inv_freq = ROPE_BASE ** (-np.arange(HEAD // 2) * 2.0 / HEAD)
+    freq = np.concatenate([inv_freq, inv_freq]).astype(np.float32).reshape(1, HEAD)
     nz = lax.axis_size("sp") // (2 * COLS)
     vmem = pl.BlockSpec(memory_space=pltpu.VMEM)
     anywhere = pl.BlockSpec(memory_space=pltpu.HBM)

time: 63.2 us -> 62.4 us (0.987)
  no operation moved by 1% of the time
where the time goes in v5:
time: 62.4 us; the launch traced here: 62.3 us
  Pallas kernels  60.9 us (98%)
  local copies, waits for them, and re-layouts  1.32 us (2%)
    pallas_call x1, Pallas kernels, body(): pl.pallas_call(functools.partial(kernel, nz), out_shape=pltpu.VMEM((ROWS,...  60.9 us
    unnamed x1, local copies, waits for them, and re-layouts  1.32 us

profile of v5, /device:TPU:193, one launch (start us, length us, event | category | flops | bytes accessed | tf_op | source)
XLA Modules:
  0.0 62.3 jit_solution(8135057278688237511)
XLA Ops:
  0.0 60.9 %shard_map.82 = bf16[128,8192]{1,0:T(8,128)(2,1)S(1)} custom-call(bf16[128,8192]{1,0:T(8,128)(2,1)} %q_hbm.1, bf16[128,1024]{1,0:T(8,128)(2,1)} %k_hbm.1, bf16[128,1024]{1,0:T(8,128)(2,1)} %v_hbm.1, f32[1,128]{1,0:T(1,128)} %bitcast.4, f32[1,128]{1,0:T(1,128)} %bitcast.5, s32[1,128]{1,0:T(1,128)} %bitcast.6, s32[1,128]{1,0:T(1,128)} %bitcast.7, ...), custom_call_target="tpu_custom_call" | custom-call | tf_op jit(solution)/shard_map/pallas_call | solution.py:463
  60.9 1.3 %copy.10 = bf16[128,8192]{1,0:T(8,128)(2,1)} copy(bf16[128,8192]{1,0:T(8,128)(2,1)S(1)} %shard_map.82) | data formatting | bytes 4194304
